TPU v7x, 32 devices: a whole 2x2x4 slice. The times are simulated.
32 devices in a mesh: row: 4 (over y, core), col: 8 (over z, x).
Axes of the slice: x: 2, y: 2, z: 4, core: 2. Of those that a mesh axis runs over, the one named last changes fastest.
Arguments:
- lhat: float32 [256, 256, 256], P(('row', 'col')), may hold values from -0.375 to 0.375
- ainv_anc: float32 [256, 256, 256], P(('row', 'col')), may hold values from -2.5 to 2.5
- diag_inv: float32 [8, 256, 256], P('col', 'row'), may hold values from -0.6 to 2, as said below
- targets: int32 [256, 1], P(('row', 'col')), may hold values from 0 to 7
Outputs:
- diag_blocks: float32 [8, 256, 256], P('col', 'row')
Inputs may be any that keep to these rules, and one draw needn't show every extreme that they name: `diag_inv`: each block is lower triangular with its diagonal entries between 0.5 and 2.
All inputs are finite; a program needn't handle non-finite values.
Results may differ from a plain program's by a relative error of at most 0.0003.
Values sent between devices are 32-bit elements; how exact they have to be, the bound alone decides.
A program may use at most 64 MiB of HBM per device.

v0:
```python
import jax
import jax.numpy as jnp
from jax import lax
from jax.sharding import PartitionSpec as P


def on_device(lhat, ainv_anc, diag_inv, targets):
    row_count = lax.axis_size("row")
    row_index = lax.axis_index("row")
    width = diag_inv.shape[2]
    row_share = width // row_count
    owned_count = diag_inv.shape[0]
    super_count = owned_count * lax.axis_size("col")
    col_start = row_index * row_share
    products = -jnp.einsum("shi,shj->sij", lhat, ainv_anc, precision=lax.Precision.HIGHEST)
    slot_ids = targets[:, 0]
    factor_piece = lax.all_gather(diag_inv, "row", axis=1, tiled=True)
    col_slice = lax.dynamic_slice_in_dim(factor_piece, col_start, row_share, 2)
    gram_rows = jnp.einsum("kia,kib->kab", col_slice, factor_piece, precision=lax.Precision.HIGHEST)
    received = lax.all_to_all(products, "row", split_axis=1, concat_axis=0, tiled=True)
    ids_all = lax.all_gather(slot_ids, "row", axis=0, tiled=True)
    labels = jnp.arange(super_count, dtype=jnp.int32)
    one_hot = (labels[:, None] == ids_all[None, :]).astype(jnp.float32)
    summed = jnp.einsum("kn,nij->kij", one_hot, received, precision=lax.Precision.HIGHEST)
    own_blocks = lax.psum_scatter(summed, "col", scatter_dimension=0, tiled=True)
    return own_blocks + gram_rows


def solution(mesh):
    placed = (
        P(("row", "col"), None, None),
        P(("row", "col"), None, None),
        P("col", "row", None),
        P(("row", "col"), None),
    )
    return jax.shard_map(
        on_device, mesh=mesh, in_specs=placed, out_specs=P("col", "row", None), check_vma=False
    )
```

profile of v0, /device:TPU:0, one launch (start us, length us, event | category | flops | bytes accessed | tf_op | source)
XLA Modules:
  0.0 122.8 jit_solution(2342706198738473607)
XLA Ops:
  6.5 0.0 copy-start
  6.5 1.6 %copy-done = f32[8,256,256]{2,1,0:T(8,128)S(1)} copy-done((f32[8,256,256]{2,1,0:T(8,128)S(1)}, f32[8,256,256]{2,1,0:T(8,128)}, u32[]{:S(2)}) %copy-start) | copy-done | bytes 2097176
  8.1 5.1 %convolution_negate_fusion = f32[8,256,256]{2,1,0:T(8,128)S(1)} fusion(f32[8,256,256]{2,1,0:T(8,128)S(1)} %copy-done, f32[8,256,256]{2,1,0:T(8,128)} %param.5), kind=kOutput, calls=%fused_computation.3 | convolution fusion | flops 1611137024 | bytes 6291456 | tf_op jit(solution)/shard_map/shi,shj->sij/dot_general | solution.py:15
  13.2 2.5 %copy.9 = f32[8,256,256]{2,0,1:T(8,128)} copy(f32[8,256,256]{2,1,0:T(8,128)S(1)} %convolution_negate_fusion) | data formatting | bytes 4194304 | tf_op jit(solution)/shard_map/neg | solution.py:15
  15.8 0.0 copy-start.3
  15.8 0.0 copy-start.2
  15.8 4.6 %all-to-all-start = ((f32[8,256,256]{2,0,1:T(8,128)}), f32[8,256,256]{2,0,1:T(8,128)}, u32[]{:S(2)}, u32[]{:S(2)}) async-start(f32[8,256,256]{2,0,1:T(8,128)} %copy.9), calls=%async_computation | async-start | bytes 4194304 | tf_op jit(solution)/shard_map/all_to_all | solution.py:20
  20.4 0.0 reduce-scatter.2.cloned.1.call-start
  20.4 0.0 copy-done.3
  20.4 0.6 dynamic-slice
  21.7 0.0 copy-done.2
  21.7 0.1 bitcast_dynamic-update-slice_fusion
  21.8 25.0 %all-reduce = s32[32]{0:T(128)S(1)} all-reduce(s32[32]{0:T(128)S(1)} %bitcast_dynamic-update-slice_fusion), channel_id=2, replica_groups=mesh['row'=4,'col'=8] {'row'}, use_global_device_ids=true, to_apply=%add | all-reduce | flops 32 | bytes 256
  46.8 0.0 all-to-all-done
  46.8 0.0 copy-start.1
  46.8 2.4 %fusion = f32[8,64,256]{2,0,1:T(8,128)S(1)} fusion(f32[8,4,64,256]{3,0,2,1:T(8,128)} %bitcast.3, s32[32]{0:T(128)S(1)} %all-reduce), kind=kOutput, calls=%fused_computation | convolution fusion | flops 50331904 | bytes 2621568 | tf_op jit(solution)/shard_map/kn,nij->kij/dot_general | solution.py:24
  49.2 1.0 copy.11
  50.2 0.0 reduce-scatter.2.cloned.1.call-update
  50.2 0.0 copy-done.1
  50.2 5.8 %all_gather.7 = f32[1,256,256]{2,1,0:T(8,128)S(1)} all-gather(f32[1,64,256]{2,1,0:T(8,128)S(1)} %copy-done.1), channel_id=1, replica_groups=mesh['row'=4,'col'=8] {'row'}, dimensions={1}, use_global_device_ids=true | all-gather | bytes 327680 | tf_op jit(solution)/shard_map/all_gather | solution.py:17
  56.0 58.1 %reduce-scatter.2.cloned.1.call-done = f32[1,64,256]{2,1,0:T(8,128)} async-done(((f32[8,64,256]{2,1,0:T(8,128)}), f32[1,64,256]{2,1,0:T(8,128)}) %reduce-scatter.2.cloned.1.call-update) | async-done | bytes 65552 | tf_op jit(solution)/shard_map/reduce_scatter | solution.py:25
  114.0 1.9 %fusion.3 = f32[1,64,256]{2,1,0:T(8,128)} fusion(f32[1,64,256]{2,1,0:T(8,128)} %reduce-scatter.2.cloned.1.call-done, f32[1,256,256]{2,1,0:T(8,128)S(1)} %all_gather.7, s32[]{:T(128)S(6)} %select_n.3), kind=kOutput, calls=%fused_computation.5 | convolution fusion | flops 50348032 | bytes 524292 | tf_op jit(solution)/shard_map/kia,kib->kab/dot_general | solution.py:19
  (1 shorter events, 0.0 us)
Async XLA Ops:
  6.5 1.6 %copy-start = (f32[8,256,256]{2,1,0:T(8,128)S(1)}, f32[8,256,256]{2,1,0:T(8,128)}, u32[]{:S(2)}) copy-start(f32[8,256,256]{2,1,0:T(8,128)} %param.4) | copy-start | bytes 6291460
  15.8 4.6 %copy-start.3 = (u32[32]{0:T(128)S(1)}, u32[32]{0:T(128)}, u32[]{:S(2)}) copy-start(u32[32]{0:T(128)} %constant.17) | copy-start | bytes 388
  15.8 5.9 %copy-start.2 = (s32[8,1]{0,1:T(1,128)S(1)}, s32[8,1]{0,1:T(1,128)}, u32[]{:S(2)}) copy-start(s32[8,1]{0,1:T(1,128)} %param.7) | copy-start | bytes 100
  15.8 31.0 %all-to-all-start = ((f32[8,256,256]{2,0,1:T(8,128)}), f32[8,256,256]{2,0,1:T(8,128)}, u32[]{:S(2)}, u32[]{:S(2)}) async-start(f32[8,256,256]{2,0,1:T(8,128)} %copy.9), calls=%async_computation | async-start | bytes 4194304 | tf_op jit(solution)/shard_map/all_to_all | solution.py:20
  20.4 93.7 %reduce-scatter.2.cloned.1.call-start = ((), (), s32[]{:S(2)}) async-start(), calls=%async_computation.2 | async-start | bytes 589824 | tf_op jit(solution)/shard_map/reduce_scatter | solution.py:25
  46.8 3.4 %copy-start.1 = (f32[1,64,256]{2,1,0:T(8,128)S(1)}, f32[1,64,256]{2,1,0:T(8,128)}, u32[]{:S(2)}) copy-start(f32[1,64,256]{2,1,0:T(8,128)} %param.6) | copy-start | bytes 196612
Sparse Core Ops, SparseCore 0:
  50.3 63.6 reduce-scatter.1
where the time goes:
time: 123 us
  waiting for transfers between devices  58.1 us (47%)
  blocking collectives  30.8 us (25%)
  between operations  14.1 us (11%)
  matrix products  9.4 us (8%)
  local copies, waits for them, and re-layouts  5.77 us (5%)
  starting transfers between devices  4.61 us (4%)
    reduce_scatter x1, waiting for transfers between devices, on_device(): lax.psum_scatter(summed, 'col', scatter_dimension=0, tiled=True)  58.1 us
    unnamed x1, blocking collectives  25 us
    all_gather x1, blocking collectives, on_device(): factor_piece = lax.all_gather(diag_inv, 'row', axis=1, tiled=True)  5.78 us
    dot_general x1, matrix products, on_device(): jnp.einsum('shi,shj->sij', lhat, ainv_anc, precision=lax.Precision.HIGHEST)  5.1 us
    all_to_all x1, starting transfers between devices, on_device(): lax.all_to_all(products, 'row', split_axis=1, concat_axis=0, tiled=True)  4.57 us
    neg x1, local copies, waits for them, and re-layouts, on_device(): -jnp.einsum('shi,shj->sij', lhat, ainv_anc, precision=lax.Precision.HIGHEST)  2.53 us
  transfers between devices with their start and end apart: 2, of which 1 were waited for; matrix products, arithmetic and copies ran while one was open for 1% of the time, Pallas kernels for 0%

commit v1 on v0

v1 whole, which is shorter than its diff:
```python
import functools

import jax
import jax.numpy as jnp
from jax import lax
from jax.experimental import pallas as pl
from jax.experimental.pallas import tpu as pltpu
from jax.sharding import PartitionSpec as P

MESH = pl.DeviceIdType.MESH
DN = (((0,), (0,)), ((), ()))


def gram_dot(a, b):
    a_hi = a.astype(jnp.bfloat16)
    a_lo = (a - a_hi.astype(jnp.float32)).astype(jnp.bfloat16)
    b_hi = b.astype(jnp.bfloat16)
    b_lo = (b - b_hi.astype(jnp.float32)).astype(jnp.bfloat16)
    left = jnp.concatenate([a_hi, a_lo, a_hi], axis=0)
    right = jnp.concatenate([b_hi, b_hi, b_lo], axis=0)
    return lax.dot_general(left, right, DN, preferred_element_type=jnp.float32)


def kernel(
    dims,
    lhat, ainv, diag, targets, out,
    lbuf, abuf, dbuf, prod, send0, own0, recv0, send1a, send1b, recv1a, recv1b,
    sum2a, sum2b, recv2a, recv2b, sum3, recv3,
    load_sem, d_sem, s0, r0, s1a, r1a, s1b, r1b, s2a, r2a, s2b, r2b, s3, r3,
):
    yn, zn, slots, share, width = dims
    half = width // 2
    row, col = lax.axis_index("row"), lax.axis_index("col")
    y, c = lax.div(row, 2), lax.rem(row, 2)
    z, x = lax.div(col, 2), lax.rem(col, 2)

    def dev(y_, c_, z_, x_):
        return {"row": y_ * 2 + c_, "col": z_ * 2 + x_}

    shifts = [zn // 2] + [d for d in range(1, zn) if d != zn // 2] if zn > 1 else []
    order = shifts + [0]
    core_peer = dev(y, 1 - c, z, x)
    x_peer = dev(y, c, z, 1 - x)
    y_ids = [lax.rem(y + d, yn) for d in range(1, yn)]
    y_peers = [dev(i, c, z, x) for i in y_ids]
    z_peers = [dev(y, c, lax.rem(z + d, zn), x) for d in shifts]
    peers = [core_peer, x_peer] + y_peers + z_peers

    loads = []
    for s in range(slots):
        pair = (
            pltpu.make_async_copy(lhat.at[s], lbuf.at[s], load_sem.at[s, 0]),
            pltpu.make_async_copy(ainv.at[s], abuf.at[s], load_sem.at[s, 1]),
        )
        for copy in pair:
            copy.start()
        loads.append(pair)
    d_load = pltpu.make_async_copy(diag.at[0], dbuf, d_sem)
    d_load.start()

    barrier = pltpu.get_barrier_semaphore()
    for peer in peers:
        pl.semaphore_signal(barrier, inc=1, device_id=peer, device_id_type=MESH)

    for s in range(slots):
        for copy in loads[s]:
            copy.wait()
        prod[s] = gram_dot(lbuf[s], abuf[s]).reshape(yn, 2, share, width)
    d_load.wait()
    prod[slots] = gram_dot(dbuf[...], dbuf[...]).reshape(yn, 2, share, width)

    def segment(o, side, dest):
        zd = lax.rem(z + order[o], zn)
        for xi in range(2):
            k = zd * 2 + xi
            weights = [jnp.where(targets[0, s] == k, -1.0, 0.0) for s in range(slots)]
            weights.append(jnp.where(col == k, 1.0, 0.0))

            def body(yo, carry):
                for h in range(2):
                    lanes = slice(h * half, (h + 1) * half)
                    total = weights[0] * prod[0, yo, side, :, lanes]
                    for s in range(1, slots + 1):
                        total = total + weights[s] * prod[s, yo, side, :, lanes]
                    dest[o, h, xi, yo] = total
                return carry

            lax.fori_loop(0, yn, body, 0)

    def remote(src, dst, send, recv, peer):
        copy = pltpu.make_async_remote_copy(
            src_ref=src, dst_ref=dst, send_sem=send, recv_sem=recv, device_id=peer, device_id_type=MESH
        )
        copy.start()
        return copy

    started = []
    copies0, copies1a, copies1b, copies2a, copies2b = {}, {}, {}, {}, {}
    copies3 = {}

    def stage0(o):
        copies0[o] = remote(send0.at[o], recv0.at[o], s0.at[o], r0.at[o], core_peer)
        started.append(copies0[o])

    def stage1(o):
        copies0[o].wait_recv()
        send1a[o] = own0[o, 0, 1 - x] + recv0[o, 0, 1 - x]
        for i, yo in enumerate(y_ids):
            for xi in range(2):
                send1b[o, i, xi] = own0[o, 1, xi, yo] + recv0[o, 1, xi, yo]
        copies1a[o] = remote(send1a.at[o], recv1a.at[o], s1a.at[o], r1a.at[o], x_peer)
        copies1b[o] = [
            remote(send1b.at[o, i], recv1b.at[o, i], s1b.at[o, i], r1b.at[o, i], peer)
            for i, peer in enumerate(y_peers)
        ]
        started.extend([copies1a[o]] + copies1b[o])

    def stage2(o):
        copies1a[o].wait_recv()
        sum2a[o] = own0[o, 0, x] + recv0[o, 0, x] + recv1a[o]
        copies2a[o] = [
            remote(sum2a.at[o, yo], recv2a.at[o, i], s2a.at[o, i], r2a.at[o, i], peer)
            for i, (yo, peer) in enumerate(zip(y_ids, y_peers))
        ]
        for copy in copies1b[o]:
            copy.wait_recv()
        for xi in range(2):
            total = own0[o, 1, xi, y] + recv0[o, 1, xi, y]
            for i in range(yn - 1):
                total = total + recv1b[o, i, xi]
            sum2b[o, xi] = total
        copies2b[o] = remote(sum2b.at[o, 1 - x], recv2b.at[o], s2b.at[o], r2b.at[o], x_peer)
        started.extend(copies2a[o] + [copies2b[o]])

    def stage3(o):
        for copy in copies2a[o]:
            copy.wait_recv()
        total = sum2a[o, y]
        for i in range(yn - 1):
            total = total + recv2a[o, i]
        sum3[o, 0] = total
        if o < zn - 1:
            first = remote(sum3.at[o, 0], recv3.at[o, 0], s3.at[o, 0], r3.at[o, 0], z_peers[o])
        copies2b[o].wait_recv()
        sum3[o, 1] = sum2b[o, x] + recv2b[o]
        if o < zn - 1:
            second = remote(sum3.at[o, 1], recv3.at[o, 1], s3.at[o, 1], r3.at[o, 1], z_peers[o])
            copies3[o] = (first, second)
            started.extend(copies3[o])

    for o in range(zn):
        segment(o, 1 - c, send0)
        if o == 0:
            pl.semaphore_wait(barrier, len(peers))
        stage0(o)
    ahead, lag = 2, 2
    for step in range(zn + ahead + lag):
        if step < zn:
            segment(step, c, own0)
            stage1(step)
        if 0 <= step - ahead < zn:
            stage2(step - ahead)
        if 0 <= step - ahead - lag < zn:
            stage3(step - ahead - lag)

    totals = [sum3[zn - 1, h] for h in range(2)]
    for o in range(zn - 1):
        for h in range(2):
            copies3[o][h].wait_recv()
            totals[h] = totals[h] + recv3[o, h]
    for h in range(2):
        out[0, :, h * half:(h + 1) * half] = totals[h]
    for copy in started:
        copy.wait_send()


def on_device(lhat, ainv, diag, targets):
    rows, cols = lax.axis_size("row"), lax.axis_size("col")
    slots, width = lhat.shape[0], lhat.shape[2]
    height = lhat.shape[1]
    yn, zn, share = rows // 2, cols // 2, diag.shape[1]
    half = width // 2
    f32, dma = jnp.float32, pltpu.SemaphoreType.DMA
    any_space = pl.BlockSpec(memory_space=pl.ANY)
    tail = (share, half)
    scratch = [
        pltpu.VMEM((slots, height, width), f32),
        pltpu.VMEM((slots, height, width), f32),
        pltpu.VMEM((share, width), f32),
        pltpu.VMEM((slots + 1, yn, 2, share, width), f32),
        pltpu.VMEM((zn, 2, 2, yn) + tail, f32),
        pltpu.VMEM((zn, 2, 2, yn) + tail, f32),
        pltpu.VMEM((zn, 2, 2, yn) + tail, f32),
        pltpu.VMEM((zn, yn) + tail, f32),
        pltpu.VMEM((zn, yn - 1, 2) + tail, f32),
        pltpu.VMEM((zn, yn) + tail, f32),
        pltpu.VMEM((zn, yn - 1, 2) + tail, f32),
        pltpu.VMEM((zn, yn) + tail, f32),
        pltpu.VMEM((zn, 2) + tail, f32),
        pltpu.VMEM((zn, yn - 1) + tail, f32),
        pltpu.VMEM((zn,) + tail, f32),
        pltpu.VMEM((zn, 2) + tail, f32),
        pltpu.VMEM((zn - 1, 2) + tail, f32),
        dma((slots, 2)), dma,
        dma((zn,)), dma((zn,)),
        dma((zn,)), dma((zn,)),
        dma((zn, yn - 1)), dma((zn, yn - 1)),
        dma((zn, yn - 1)), dma((zn, yn - 1)),
        dma((zn,)), dma((zn,)),
        dma((zn - 1, 2)), dma((zn - 1, 2)),
    ]
    return pl.pallas_call(
        functools.partial(kernel, (yn, zn, slots, share, width)),
        out_shape=jax.ShapeDtypeStruct(diag.shape, f32),
        in_specs=[any_space, any_space, any_space, pl.BlockSpec(memory_space=pltpu.SMEM)],
        out_specs=pl.BlockSpec(memory_space=pltpu.VMEM),
        scratch_shapes=scratch,
        compiler_params=pltpu.CompilerParams(
            collective_id=0, has_side_effects=True, vmem_limit_bytes=60 * 1024 * 1024
        ),
    )(lhat, ainv, diag, targets.T)


def solution(mesh):
    placed = (
        P(("row", "col"), None, None),
        P(("row", "col"), None, None),
        P("col", "row", None),
        P(("row", "col"), None),
    )
    return jax.shard_map(
        on_device, mesh=mesh, in_specs=placed, out_specs=P("col", "row", None), check_vma=False
    )
```

time: 123 us -> 26.9 us (0.22)
  waiting for transfers between devices: 58.1 us -> 0 us
  blocking collectives: 30.8 us -> 0 us
  Pallas kernels: 0 us -> 25.2 us
  between operations: 14.1 us -> 0.01 us
  matrix products: 9.4 us -> 0 us
  starting transfers between devices: 4.61 us -> 0 us
  local copies, waits for them, and re-layouts: 5.77 us -> 1.47 us
    reduce_scatter x1 -> x0, waiting for transfers between devices: 58.1 us -> none  [on_device(): lax.psum_scatter(summed, 'col', scatter_dimension=0, tiled=True)]
    pallas_call x0 -> x1, Pallas kernels: none -> 25.2 us  [on_device(): pl.pallas_call(functools.partial(kernel, (yn, zn, slots, share, width)),...]
    unnamed x1 -> x0, blocking collectives: 25 us -> none
    dot_general x3 -> x0, matrix products: 9.4 us -> none  [the longest x1 5.1 us: on_device(): jnp.einsum('shi,shj->sij', lhat, ainv_anc, precision=lax.Precision.HIGHEST)]
    all_gather x1 -> x0, blocking collectives: 5.78 us -> none  [on_device(): factor_piece = lax.all_gather(diag_inv, 'row', axis=1, tiled=True)]
    all_to_all x1 -> x0, starting transfers between devices: 4.57 us -> none  [on_device(): lax.all_to_all(products, 'row', split_axis=1, concat_axis=0, tiled=True)]
    neg x1 -> x0, local copies, waits for them, and re-layouts: 2.53 us -> none  [on_device(): -jnp.einsum('shi,shj->sij', lhat, ainv_anc, precision=lax.Precision.HIGHEST)]
  transfers between devices with their start and end apart: 2 -> 0, of which waited for: 1 -> 0; matrix products, arithmetic and copies ran while one was open for 1% -> 0% of each run, Pallas kernels for 0% -> 0%
where the time goes in v1:
time: 26.9 us; the launch traced here: 26.7 us
  Pallas kernels  25.2 us (94%)
  local copies, waits for them, and re-layouts  1.47 us (5%)
    pallas_call x1, Pallas kernels, on_device(): pl.pallas_call(functools.partial(kernel, (yn, zn, slots, share, width)),...  25.2 us
    unnamed x1, local copies, waits for them, and re-layouts  1.47 us

profile of v1, /device:TPU:0, one launch (start us, length us, event | category | flops | bytes accessed | tf_op | source)
XLA Modules:
  0.0 26.7 jit_solution(15434039096403791538)
XLA Ops:
  0.0 25.2 %shard_map.46 = f32[1,64,256]{2,1,0:T(8,128)} custom-call(f32[8,256,256]{2,1,0:T(8,128)} %lhat.1, f32[8,256,256]{2,1,0:T(8,128)} %ainv.1, f32[1,64,256]{2,1,0:T(8,128)} %diag.1, s32[1,8]{1,0:T(1,128)} %bitcast.1), custom_call_target="tpu_custom_call" | custom-call | tf_op jit(solution)/shard_map/pallas_call | solution.py:212
  25.2 1.5 %copy.6 = f32[1,64,256]{2,1,0:T(8,128)} copy(f32[1,64,256]{2,1,0:T(8,128)} %shard_map.46) | data formatting | bytes 131072

commit v2 on v1

--- a/solution.py
+++ b/solution.py
@@ -23,10 +23,10 @@
 
 def kernel(
     dims,
-    lhat, ainv, diag, targets, out,
-    lbuf, abuf, dbuf, prod, send0, own0, recv0, send1a, send1b, recv1a, recv1b,
+    lhat, ainv, diag, targets_in, out,
+    targets, lbuf, abuf, dbuf, prod, send0, own0, recv0, send1a, send1b, recv1a, recv1b,
     sum2a, sum2b, recv2a, recv2b, sum3, recv3,
-    load_sem, d_sem, s0, r0, s1a, r1a, s1b, r1b, s2a, r2a, s2b, r2b, s3, r3,
+    load_sem, d_sem, t_sem, s0, r0, s1a, r1a, s1b, r1b, s2a, r2a, s2b, r2b, s3, r3,
 ):
     yn, zn, slots, share, width = dims
     half = width // 2
@@ -46,6 +46,8 @@
     z_peers = [dev(y, c, lax.rem(z + d, zn), x) for d in shifts]
     peers = [core_peer, x_peer] + y_peers + z_peers
 
+    t_load = pltpu.make_async_copy(targets_in, targets, t_sem)
+    t_load.start()
     loads = []
     for s in range(slots):
         pair = (
@@ -67,6 +69,7 @@
             copy.wait()
         prod[s] = gram_dot(lbuf[s], abuf[s]).reshape(yn, 2, share, width)
     d_load.wait()
+    t_load.wait()
     prod[slots] = gram_dot(dbuf[...], dbuf[...]).reshape(yn, 2, share, width)
 
     def segment(o, side, dest):
@@ -181,9 +184,9 @@
     yn, zn, share = rows // 2, cols // 2, diag.shape[1]
     half = width // 2
     f32, dma = jnp.float32, pltpu.SemaphoreType.DMA
-    any_space = pl.BlockSpec(memory_space=pl.ANY)
     tail = (share, half)
     scratch = [
+        pltpu.SMEM((1, slots), jnp.int32),
         pltpu.VMEM((slots, height, width), f32),
         pltpu.VMEM((slots, height, width), f32),
         pltpu.VMEM((share, width), f32),
@@ -201,7 +204,7 @@
         pltpu.VMEM((zn,) + tail, f32),
         pltpu.VMEM((zn, 2) + tail, f32),
         pltpu.VMEM((zn - 1, 2) + tail, f32),
-        dma((slots, 2)), dma,
+        dma((slots, 2)), dma, dma,
         dma((zn,)), dma((zn,)),
         dma((zn,)), dma((zn,)),
         dma((zn, yn - 1)), dma((zn, yn - 1)),
@@ -211,8 +214,8 @@
     ]
     return pl.pallas_call(
         functools.partial(kernel, (yn, zn, slots, share, width)),
-        out_shape=jax.ShapeDtypeStruct(diag.shape, f32),
-        in_specs=[any_space, any_space, any_space, pl.BlockSpec(memory_space=pltpu.SMEM)],
+        out_shape=pltpu.VMEM(diag.shape, f32),
+        in_specs=[pl.BlockSpec(memory_space=pltpu.HBM)] * 4,
         out_specs=pl.BlockSpec(memory_space=pltpu.VMEM),
         scratch_shapes=scratch,
         compiler_params=pltpu.CompilerParams(

time: 26.9 us -> 24.8 us (0.922)
  Pallas kernels: 25.2 us -> 24 us
  local copies, waits for them, and re-layouts: 1.47 us -> 0.63 us
    pallas_call x1, Pallas kernels: 25.2 us -> 24 us  [on_device(): pl.pallas_call(functools.partial(kernel, (yn, zn, slots, share, width)),...]
    unnamed x1, local copies, waits for them, and re-layouts: 1.47 us -> 0.63 us
where the time goes in v2:
time: 24.8 us; the launch traced here: 24.6 us
  Pallas kernels  24 us (97%)
  local copies, waits for them, and re-layouts  0.63 us (3%)
    pallas_call x1, Pallas kernels, on_device(): pl.pallas_call(functools.partial(kernel, (yn, zn, slots, share, width)),...  24 us
    unnamed x1, local copies, waits for them, and re-layouts  0.63 us

profile of v2, /device:TPU:0, one launch (start us, length us, event | category | flops | bytes accessed | tf_op | source)
XLA Modules:
  0.0 24.6 jit_solution(15211120145947052621)
XLA Ops:
  0.0 24.0 %shard_map.46 = f32[1,64,256]{2,1,0:T(8,128)S(1)} custom-call(f32[8,256,256]{2,1,0:T(8,128)} %lhat.1, f32[8,256,256]{2,1,0:T(8,128)} %ainv.1, f32[1,64,256]{2,1,0:T(8,128)} %diag.1, s32[1,8]{1,0:T(1,128)} %bitcast.1), custom_call_target="tpu_custom_call" | custom-call | tf_op jit(solution)/shard_map/pallas_call | solution.py:215
  24.0 0.6 %copy.6 = f32[1,64,256]{2,1,0:T(8,128)} copy(f32[1,64,256]{2,1,0:T(8,128)S(1)} %shard_map.46) | data formatting | bytes 131072

commit v3 on v2

--- a/solution.py
+++ b/solution.py
@@ -48,6 +48,8 @@
 
     t_load = pltpu.make_async_copy(targets_in, targets, t_sem)
     t_load.start()
+    d_load = pltpu.make_async_copy(diag.at[0], dbuf, d_sem)
+    d_load.start()
     loads = []
     for s in range(slots):
         pair = (
@@ -57,20 +59,18 @@
         for copy in pair:
             copy.start()
         loads.append(pair)
-    d_load = pltpu.make_async_copy(diag.at[0], dbuf, d_sem)
-    d_load.start()
 
     barrier = pltpu.get_barrier_semaphore()
     for peer in peers:
         pl.semaphore_signal(barrier, inc=1, device_id=peer, device_id_type=MESH)
 
+    d_load.wait()
+    prod[slots] = gram_dot(dbuf[...], dbuf[...]).reshape(yn, 2, share, width)
     for s in range(slots):
         for copy in loads[s]:
             copy.wait()
         prod[s] = gram_dot(lbuf[s], abuf[s]).reshape(yn, 2, share, width)
-    d_load.wait()
     t_load.wait()
-    prod[slots] = gram_dot(dbuf[...], dbuf[...]).reshape(yn, 2, share, width)
 
     def segment(o, side, dest):
         zd = lax.rem(z + order[o], zn)
@@ -88,7 +88,7 @@
                     dest[o, h, xi, yo] = total
                 return carry
 
-            lax.fori_loop(0, yn, body, 0)
+            lax.fori_loop(0, yn, body, 0, unroll=yn <= 2)
 
     def remote(src, dst, send, recv, peer):
         copy = pltpu.make_async_remote_copy(

time: 24.8 us -> 25.8 us (1.040)
  Pallas kernels: 24 us -> 25.1 us
    pallas_call x1, Pallas kernels: 24 us -> 25.1 us  [on_device(): pl.pallas_call(functools.partial(kernel, (yn, zn, slots, share, width)),...]
where the time goes in v3:
time: 25.8 us; the launch traced here: 25.7 us
  Pallas kernels  25.1 us (97%)
  local copies, waits for them, and re-layouts  0.63 us (2%)
    pallas_call x1, Pallas kernels, on_device(): pl.pallas_call(functools.partial(kernel, (yn, zn, slots, share, width)),...  25.1 us
    unnamed x1, local copies, waits for them, and re-layouts  0.63 us

profile of v3, /device:TPU:0, one launch (start us, length us, event | category | flops | bytes accessed | tf_op | source)
XLA Modules:
  0.0 25.7 jit_solution(10118601941291348347)
XLA Ops:
  0.0 25.1 %shard_map.46 = f32[1,64,256]{2,1,0:T(8,128)S(1)} custom-call(f32[8,256,256]{2,1,0:T(8,128)} %lhat.1, f32[8,256,256]{2,1,0:T(8,128)} %ainv.1, f32[1,64,256]{2,1,0:T(8,128)} %diag.1, s32[1,8]{1,0:T(1,128)} %bitcast.1), custom_call_target="tpu_custom_call" | custom-call | tf_op jit(solution)/shard_map/pallas_call | solution.py:215
  25.1 0.6 %copy.6 = f32[1,64,256]{2,1,0:T(8,128)} copy(f32[1,64,256]{2,1,0:T(8,128)S(1)} %shard_map.46) | data formatting | bytes 131072
